TPU v7x, 32 devices: a 4x4x1 block of a 4x4x8 slice. The times are simulated.
32 devices in a mesh: dp: 1 (over z), ep: 32 (over y, x, core).
Axes of the slice: x: 4, y: 4, z: 1, core: 2. Of those that a mesh axis runs over, the one named last changes fastest.
The devices are a block of a 4x4x8 slice.
Arguments:
- hidden: bfloat16 [8192, 2048], P(('dp', 'ep'))
- norm_gain: bfloat16 [2048], replicated
- w_gate: bfloat16 [2048, 64], replicated
- w1_shared: bfloat16 [2048, 2816], replicated
- w3_shared: bfloat16 [2048, 2816], replicated
- w2_shared: bfloat16 [2816, 2048], replicated
- w1_experts: bfloat16 [64, 2048, 1408], P('ep')
- w3_experts: bfloat16 [64, 2048, 1408], P('ep')
- w2_experts: bfloat16 [64, 1408, 2048], P('ep')
- topk_ids: int32 [8192, 6], P(('dp', 'ep'))
Outputs:
- output: bfloat16 [8192, 2048], P(('dp', 'ep'))
All inputs are finite; a program needn't handle non-finite values.
Results may differ from a plain program's by a relative error of at most 0.00588174.
Values are sent between devices in bfloat16 or wider.
A program may use at most 768 MiB of HBM per device.

v0:
```python
import functools

import jax
import jax.numpy as jnp
from jax import lax
from jax.experimental import pallas as pl
from jax.experimental.pallas import tpu as pltpu
from jax.sharding import PartitionSpec as P

ROUTE_SCALE = 16
NORM_EPS = 1e-6
QUAD = 4
MESH = pl.DeviceIdType.MESH


def rms_norm(hidden, norm_gain):
    rows_f = hidden.astype(jnp.float32)
    inv_rms = lax.rsqrt(jnp.mean(rows_f * rows_f, axis=-1, keepdims=True) + NORM_EPS)
    return (rows_f * inv_rms * norm_gain.astype(jnp.float32)).astype(jnp.bfloat16)


def swiglu(rows_in, w_up, w_lin, w_down):
    gate_act = jnp.dot(rows_in, w_up, preferred_element_type=jnp.float32)
    lin_act = jnp.dot(rows_in, w_lin, preferred_element_type=jnp.float32)
    inner_act = (jax.nn.silu(gate_act) * lin_act).astype(jnp.bfloat16)
    return jnp.dot(inner_act, w_down, preferred_element_type=jnp.float32).astype(jnp.bfloat16)


def assign_slots(mask, cap_e):
    rows = mask.shape[-3]
    before = (jnp.arange(rows)[:, None] > jnp.arange(rows)[None, :]).astype(jnp.bfloat16)
    rank = jnp.einsum('ut,...tde->...ude', before, mask.astype(jnp.bfloat16), preferred_element_type=jnp.float32)
    total = jnp.sum(mask, axis=-3)
    count = jnp.minimum(total, cap_e)
    local = mask.shape[-1]
    later = (jnp.arange(local)[:, None] < jnp.arange(local)[None, :]).astype(jnp.float32)
    start = jnp.sum(count[..., :, None] * later, axis=-2)
    return rank, total, count, start


def flow_table(n):
    side = next(s for s in range(1, n + 1) if 2 * s * s >= n)
    flows = [(2, 2, 0), (2, 2, 1), (1, 3, 0), (3, 1, 0),
             (2, 0, 0), (2, 0, 1), (0, 2, 0), (0, 2, 1),
             (2, 1, 0), (2, 1, 1), (1, 2, 0), (1, 2, 1),
             (2, 3, 0), (2, 3, 1), (3, 2, 0), (3, 2, 1),
             (1, 0, 0), (3, 0, 0), (0, 1, 0), (0, 3, 0),
             (1, 0, 1), (3, 0, 1), (0, 1, 1), (0, 3, 1),
             (1, 1, 0), (3, 3, 0), (1, 1, 1), (3, 3, 1),
             (1, 3, 1), (3, 1, 1), (0, 0, 1), (0, 0, 0)]
    assert len(set(flows)) == n and side == 4
    relays = {}
    for i, (dx, dy, dc) in enumerate(flows):
        if 2 in (dx, dy):
            turn = 3 if dc else 1
            relays[i] = (turn if dx == 2 else 0, turn if dy == 2 else 0)
    return side, flows, relays


def device_at(me, side, step, sign=1):
    dx, dy, dc = step
    col, line = (me // 2) % side, me // (2 * side)
    col = (col + sign * dx + side) % side
    line = (line + sign * dy + side) % side
    return (line * side + col) * 2 + (me + dc) % 2


def moe_kernel(n, cap_e, cap, rows_ref, pick_ref, pack_ref, comb_ref, w1_ref, w3_ref, w2_ref,
               sum_ref, recv_ref, relay_ref,
               w1_v, w3_v, w2_v, row_v, xy_v, h_v, stage_v, w_sem, row_sem, send_sem, recv_sem, relay_sem, pass_sem, got_sem):
    side, flows, relays = flow_table(n)
    relay_slot = {i: j for j, i in enumerate(relays)}
    tiles = n // QUAD
    local, depth, inner = w1_ref.shape
    block = rows_ref.shape[1]
    me = lax.axis_index('ep')

    loads = []
    for e in range(local):
        for j, (src, dst) in enumerate(((w1_ref, w1_v), (w3_ref, w3_v), (w2_ref, w2_v))):
            loads.append(pltpu.make_async_copy(src.at[e], dst.at[e], w_sem.at[3 * e + j]))

    def row_start(t):
        for q in range(QUAD):
            peer = device_at(me, side, flows[t * QUAD + q])
            pltpu.make_async_copy(rows_ref.at[peer], row_v.at[t % 2, q], row_sem.at[t % 2, q]).start()

    def staged(t, q):
        return stage_v.at[t % 2, q]

    def send_copy(t, q):
        i = t * QUAD + q
        if i in relays:
            ax, ay = relays[i]
            j = relay_slot[i]
            dst, sem, to = relay_ref.at[j], relay_sem.at[j], device_at(me, side, (ax, ay, 0))
        else:
            dst, sem, to = recv_ref.at[i], recv_sem.at[i], device_at(me, side, flows[i])
        return pltpu.make_async_remote_copy(
            src_ref=staged(t, q), dst_ref=dst, send_sem=send_sem.at[t % 2, q], recv_sem=sem,
            device_id={'ep': to}, device_id_type=MESH)

    def pass_copy(i):
        (ax, ay), (dx, dy, dc), j = relays[i], flows[i], relay_slot[i]
        return pltpu.make_async_remote_copy(
            src_ref=relay_ref.at[j], dst_ref=recv_ref.at[i], send_sem=pass_sem.at[j], recv_sem=recv_sem.at[i],
            device_id={'ep': device_at(me, side, (dx - ax + side, dy - ay + side, dc))}, device_id_type=MESH)

    def self_copy(t, q):
        return pltpu.make_async_copy(staged(t, q), recv_ref.at[t * QUAD + q], recv_sem.at[t * QUAD + q])

    row_start(0)
    for load in loads:
        load.start()

    barrier = pltpu.get_barrier_semaphore()
    for off in range(1, n):
        pl.semaphore_signal(barrier, inc=1, device_id={'ep': (me + off) % n}, device_id_type=MESH)
    pl.semaphore_wait(barrier, n - 1)

    def columns(i, width):
        return pl.ds(pl.multiple_of(i * width, width), width)

    def tile(k, carry):
        slot = k % 2
        for t in range(tiles - 1):
            @pl.when(k == t)
            def _():
                row_start(t + 1)

        for q in range(QUAD):
            pltpu.make_async_copy(rows_ref.at[0], row_v.at[slot, q], row_sem.at[slot, q]).wait()
            width = min(512, depth)
            pick = pick_ref[k * QUAD + q]

            def gather(i, carry):
                got = jnp.dot(pick, row_v[slot, q, :, columns(i, width)], preferred_element_type=jnp.float32)
                got = got.astype(jnp.bfloat16)
                for e in range(local):
                    xy_v[e, q * cap_e:(q + 1) * cap_e, columns(i, width)] = got[e * cap_e:(e + 1) * cap_e]
                return carry

            lax.fori_loop(0, depth // width, gather, 0)

        for e in range(local):
            @pl.when(k == 0)
            def _():
                loads[3 * e].wait()
                loads[3 * e + 1].wait()

            def up_cols(at):
                rows_in = xy_v[e]
                gate_act = jnp.dot(rows_in, w1_v[e, :, at], preferred_element_type=jnp.float32)
                lin_act = jnp.dot(rows_in, w3_v[e, :, at], preferred_element_type=jnp.float32)
                h_v[:, at] = (jax.nn.silu(gate_act) * lin_act).astype(jnp.bfloat16)

            def up(i, carry):
                up_cols(columns(i, 256))
                return carry

            lax.fori_loop(0, inner // 256, up, 0)
            if inner % 256:
                up_cols(pl.ds(inner - inner % 256, inner % 256))

            @pl.when(k == 0)
            def _():
                loads[3 * e + 2].wait()

            def down(i, carry):
                at = columns(i, 256)
                got = jnp.dot(h_v[...], w2_v[e, :, at], preferred_element_type=jnp.float32).astype(jnp.bfloat16)
                for q in range(QUAD):
                    row = q * local * cap_e + e * cap_e
                    xy_v[local + row // (QUAD * cap_e), row % (QUAD * cap_e):row % (QUAD * cap_e) + cap_e, at] = got[q * cap_e:(q + 1) * cap_e]
                return carry

            lax.fori_loop(0, depth // 256, down, 0)

        for t in range(3, tiles):
            ready = [i for i in relays if i // QUAD == t - 3]
            if ready:
                @pl.when(k == t)
                def _():
                    for i in ready:
                        pltpu.make_async_copy(
                            relay_ref.at[relay_slot[i]], relay_ref.at[relay_slot[i]], relay_sem.at[relay_slot[i]]).wait()
                        pass_copy(i).start()

        @pl.when(k >= 2)
        def _():
            for q in range(QUAD):
                pltpu.make_async_copy(stage_v.at[slot, q], stage_v.at[slot, q], send_sem.at[slot, q]).wait()

        for q in range(QUAD):
            width = min(512, depth)
            pack = pack_ref[k * QUAD + q]
            row = q * local * cap_e

            def compact(i, carry):
                at = columns(i, width)
                y_in = xy_v[local + row // (QUAD * cap_e), row % (QUAD * cap_e):row % (QUAD * cap_e) + local * cap_e, at]
                got = jnp.dot(pack, y_in, preferred_element_type=jnp.float32)
                stage_v[slot, q, :, at] = got.astype(jnp.bfloat16)
                return carry

            lax.fori_loop(0, depth // width, compact, 0)

        for t in range(tiles):
            @pl.when(k == t)
            def _():
                for q in range(QUAD):
                    if flows[t * QUAD + q] == (0, 0, 0):
                        self_copy(t, q).start()
                    else:
                        send_copy(t, q).start()
        return carry

    lax.fori_loop(0, tiles, tile, 0)

    slots = 2 * local
    chunks = n // 2

    def got_copy(c, j):
        return pltpu.make_async_copy(recv_ref.at[2 * c + j], xy_v.at[c % slots, pl.ds(j * cap, cap), :], got_sem.at[c % slots, j])

    def add_chunk(c, first):
        for j in range(2):
            got_copy(c, j).wait()

        def add(i, carry):
            at = columns(i, 256)
            got = jnp.dot(comb_ref[c], xy_v[c % slots, :2 * cap, at], preferred_element_type=jnp.float32)
            got = got[:block] + (got[block:2 * block] + got[2 * block:])
            sum_ref[:, at] = got if first else sum_ref[:, at] + got
            return carry

        lax.fori_loop(0, depth // 256, add, 0)

    def fetch(c):
        for j in range(2):
            pltpu.make_async_copy(recv_ref.at[2 * c + j], recv_ref.at[2 * c + j], recv_sem.at[2 * c + j]).wait()
            got_copy(c, j).start()

    fetch(0)
    fetch(1)
    add_chunk(0, True)

    def step(c, carry):
        fetch(c + 1)
        add_chunk(c, False)
        return carry

    lax.fori_loop(1, chunks - 1, step, 0)
    add_chunk(chunks - 1, False)

    for i in relays:
        pltpu.make_async_copy(relay_ref.at[relay_slot[i]], relay_ref.at[relay_slot[i]], pass_sem.at[relay_slot[i]]).wait()
    for t in range(tiles - 2, tiles):
        for q in range(QUAD):
            if flows[t * QUAD + q] != (0, 0, 0):
                pltpu.make_async_copy(staged(t, q), staged(t, q), send_sem.at[t % 2, q]).wait()


def expert_exchange(n, cap_e, cap, rows, pick, pack, comb, w1, w3, w2):
    local, depth, inner = w1.shape
    block = rows.shape[1]
    assert n % (2 * QUAD) == 0 and block >= QUAD * cap_e and 2 * cap <= QUAD * cap_e and local * 2 == QUAD
    vmem = pl.BlockSpec(memory_space=pltpu.VMEM)
    anyspec = pl.BlockSpec(memory_space=pl.ANY)
    flops = 2 * n * local * cap_e * depth * inner * 3
    passing = len(flow_table(n)[2])
    return pl.pallas_call(
        functools.partial(moe_kernel, n, cap_e, cap),
        out_shape=(jax.ShapeDtypeStruct((block, depth), jnp.float32),
                   jax.ShapeDtypeStruct((n, cap, depth), jnp.bfloat16),
                   jax.ShapeDtypeStruct((passing, cap, depth), jnp.bfloat16)),
        in_specs=[anyspec, vmem, vmem, vmem, anyspec, anyspec, anyspec],
        out_specs=(vmem, anyspec, anyspec),
        scratch_shapes=[
            pltpu.VMEM(w1.shape, jnp.bfloat16),
            pltpu.VMEM(w3.shape, jnp.bfloat16),
            pltpu.VMEM(w2.shape, jnp.bfloat16),
            pltpu.VMEM((2, QUAD, block, depth), jnp.bfloat16),
            pltpu.VMEM((2 * local, QUAD * cap_e, depth), jnp.bfloat16),
            pltpu.VMEM((QUAD * cap_e, inner), jnp.bfloat16),
            pltpu.VMEM((2, QUAD, cap, depth), jnp.bfloat16),
            pltpu.SemaphoreType.DMA((3 * local,)),
            pltpu.SemaphoreType.DMA((2, QUAD)),
            pltpu.SemaphoreType.DMA((2, QUAD)),
            pltpu.SemaphoreType.DMA((n,)),
            pltpu.SemaphoreType.DMA((passing,)),
            pltpu.SemaphoreType.DMA((passing,)),
            pltpu.SemaphoreType.DMA((2 * local, 2)),
        ],
        compiler_params=pltpu.CompilerParams(collective_id=0, has_side_effects=True, vmem_limit_bytes=67_000_000),
        cost_estimate=pl.CostEstimate(flops=flops, bytes_accessed=80_000_000, transcendentals=0),
        name='moe_exchange',
    )(rows, pick, pack, comb, w1, w3, w2)[0]


def split3(x):
    hi = lax.reduce_precision(x, 8, 7)
    mid = lax.reduce_precision(x - hi, 8, 7)
    low = (x - hi) - mid
    return [part.astype(jnp.bfloat16) for part in (hi, mid, low)]


def solution(mesh):
    n = mesh.shape['ep']
    tok_spec = P(('dp', 'ep'), None)
    expert_spec = P('ep', None, None)

    def local_fn(hidden, norm_gain, w_gate, w1_shared, w3_shared, w2_shared, w1_experts, w3_experts, w2_experts, topk_ids):
        block, depth = hidden.shape
        local = w1_experts.shape[0]
        cap_e = block // 4
        cap = block * 3 // 8
        normed = rms_norm(hidden, norm_gain)
        all_rows = lax.all_gather(normed, 'ep', axis=0, tiled=True)
        all_ids = lax.all_gather(topk_ids, 'ep', axis=0, tiled=True)

        me = lax.axis_index('ep')
        side, flows, _ = flow_table(n)
        steps = tuple(jnp.array([flow[i] for flow in flows]) for i in range(3))
        dest = device_at(me, side, steps)
        src = device_at(me, side, steps, -1)
        experts = jnp.arange(n * local)
        from_experts = (src[:, None] * local + jnp.arange(local)).reshape(-1)

        gate_perm = jnp.dot(w_gate, (experts[:, None] == from_experts).astype(jnp.bfloat16), preferred_element_type=jnp.float32).astype(jnp.bfloat16)
        gate_probs = jax.nn.softmax(jnp.dot(normed, gate_perm, preferred_element_type=jnp.float32), axis=-1)
        own_mask = jnp.any(topk_ids[:, :, None] == from_experts, axis=1).astype(jnp.float32)
        own_wts = (ROUTE_SCALE * gate_probs * own_mask).reshape(block, n, local)
        own_mask = own_mask.reshape(block, n, local)
        rank, _, _, start = assign_slots(own_mask, cap_e)
        slot = jnp.where((own_mask > 0) & (rank < cap_e), rank + start, -1.0)
        slot, own_wts = slot.transpose(1, 2, 0), own_wts.transpose(1, 2, 0)
        comb = jnp.sum(jnp.where(slot[:, :, :, None] == jnp.arange(cap, dtype=jnp.float32), own_wts[:, :, :, None], 0.0), axis=1)
        comb = comb.reshape(n // 2, 2, block, cap).transpose(0, 2, 1, 3).reshape(n // 2, block, 2 * cap)
        comb3 = jnp.concatenate(split3(comb), axis=1)
        shared_out = swiglu(normed, w1_shared, w3_shared, w2_shared)

        order = (dest[:, None] == jnp.arange(n)).astype(jnp.bfloat16)
        ids_f = jnp.dot(order, all_ids.reshape(n, -1).astype(jnp.bfloat16), preferred_element_type=jnp.float32).reshape(n, block, -1)
        local_ids = me * local + jnp.arange(local)
        mask = jnp.any(ids_f[:, :, :, None] == local_ids.astype(jnp.float32), axis=2).astype(jnp.float32)
        rank_l, _, count_l, start_l = assign_slots(mask[:, :, None, :], cap_e)
        rank_l, count_l, start_l = rank_l[:, :, 0], count_l[:, 0], start_l[:, 0]
        place = jnp.arange(cap_e, dtype=jnp.float32)
        pick = ((mask.transpose(0, 2, 1)[:, :, None, :] > 0) & (rank_l.transpose(0, 2, 1)[:, :, None, :] == place[:, None]))
        pick = pick.astype(jnp.bfloat16).reshape(n, local * cap_e, block)
        pack = ((jnp.arange(cap, dtype=jnp.float32)[:, None, None] == start_l[:, None, :, None] + place) & (place < count_l[:, None, :, None]))
        pack = pack.astype(jnp.bfloat16).reshape(n, cap, local * cap_e)

        ids_b = all_ids.reshape(n, block, -1)
        totals = jnp.sum(jnp.any(ids_b[:, :, :, None] == experts, axis=2).astype(jnp.float32), axis=1).reshape(n, n, local)
        over = jnp.any(totals > cap_e) | jnp.any(jnp.sum(jnp.minimum(totals, cap_e), axis=-1) > cap)

        pick, pack, comb3, shared_out = lax.optimization_barrier((pick, pack, comb3, shared_out))
        routed = expert_exchange(n, cap_e, cap, all_rows.reshape(n, block, depth), pick, pack, comb3, w1_experts, w3_experts, w2_experts)

        def correction(rows, row_ids, w1, w3, w2):
            probs = jax.nn.softmax(jnp.dot(normed, w_gate, preferred_element_type=jnp.float32), axis=-1)
            wts = lax.all_gather(ROUTE_SCALE * jnp.take_along_axis(probs, topk_ids, axis=1), 'ep', axis=0, tiled=True)
            row_w = jnp.sum(jnp.where(row_ids[:, :, None] == local_ids, wts[:, :, None], 0.0), axis=1)
            mask = jnp.any(row_ids[:, :, None] == local_ids, axis=1).astype(jnp.float32).reshape(n, block, 1, local)
            rank, _, _, start = assign_slots(mask, cap_e)
            left = (mask > 0) & ~((rank < cap_e) & (rank + start[:, None] < cap))
            row_w = jnp.where(left.reshape(n * block, local), row_w, 0.0)
            chunks = 16

            def step(chunk):
                r, w = chunk
                acc = jnp.zeros(r.shape, jnp.float32)
                for e in range(local):
                    acc = acc + w[:, e:e + 1] * swiglu(r, w1[e], w3[e], w2[e]).astype(jnp.float32)
                return acc

            part = lax.map(step, (rows.reshape(chunks, -1, depth), row_w.reshape(chunks, -1, local))).reshape(n * block, depth)
            return lax.psum_scatter(part, 'ep', scatter_dimension=0, tiled=True)

        def finish(total):
            return (hidden.astype(jnp.float32) + shared_out.astype(jnp.float32) + total).astype(jnp.bfloat16)

        return lax.cond(over, lambda *args: finish(routed + correction(*args)), lambda *args: finish(routed),
                        all_rows, all_ids, w1_experts, w3_experts, w2_experts)

    return jax.shard_map(local_fn, mesh=mesh, in_specs=(tok_spec, P(), P(), P(), P(), P(), expert_spec, expert_spec, expert_spec, tok_spec), out_specs=tok_spec, check_vma=False)
```

profile of v0, /device:TPU:97, one launch (start us, length us, event | category | flops | bytes accessed | tf_op | source)
XLA Modules:
  0.0 381.8 jit_solution(1571096679149042823)
XLA Ops:
  6.6 0.7 convert_element_type.177
  7.4 1.5 fusion.80
  8.9 2.5 fusion.82
  11.8 1.8 fusion.116
  14.6 1.0 select_reduce_fusion
  15.6 2.0 bitcast_reduce-precision_fusion
  17.6 4.9 %copy.98 = f32[16,256,192]{2,1,0:T(8,128)} copy(f32[16,256,192]{1,2,0:T(8,128)} %bitcast_reduce-precision_fusion) | data formatting | bytes 6291456 | tf_op jit(solution)/shard_map/reduce_precision | solution.py:302
  22.5 3.4 copy.99
  26.0 34.1 %all_gather.9 = s32[8192,6]{0,1:T(8,128)S(1)} all-gather(s32[256,6]{0,1:T(8,128)S(1)} %copy-done.7), channel_id=1, replica_groups=mesh['dp'=1,'ep'=32] {'ep'}, dimensions={0}, use_global_device_ids=true | all-gather | bytes 202752 | tf_op jit(solution)/shard_map/all_gather | solution.py:320
  60.1 1.1 copy.87
  61.2 3.3 convert_element_type.180
  66.5 2.1 fusion.78.pick_ref
  68.6 1.2 fusion.85.pack_ref
  69.8 6.1 %reduce-precision_convert_fusion = (bf16[16,256,192]{2,1,0:T(8,128)(2,1)S(1)}, bf16[16,256,192]{2,1,0:T(8,128)(2,1)S(1)}, bf16[16,256,192]{2,1,0:T(8,128)(2,1)S(1)}) fusion(f32[16,256,192]{2,1,0:T(8,128)} %copy.99, f32[16,256,192]{2,1,0:T(8,128)} %copy.98), kind=kLoop, calls=%fused_computation.75 | loop fusion | flops 4718592 | bytes 11010048 | tf_op jit(solution)/shard_map/convert_element_type | solution.py:305
  75.9 6.2 %pad_maximum_fusion.comb_ref = bf16[16,768,192]{2,1,0:T(8,128)(2,1)} fusion(bf16[16,256,192]{2,1,0:T(8,128)(2,1)S(1)} %get-tuple-element.236, bf16[16,256,192]{2,1,0:T(8,128)(2,1)S(1)} %get-tuple-element.235, bf16[16,256,192]{2,1,0:T(8,128)(2,1)S(1)} %get-tuple-element.237), kind=kLoop, calls=%fused_computation.71 | loop fusion | flops 14155776 | bytes 9437184 | tf_op jit(solution)/shard_map/concatenate | solution.py:340
  82.2 4.8 %fusion.117 = f32[256,2816]{1,0:T(8,128)} fusion(bf16[256,2048]{1,0:T(8,128)(2,1)S(1)} %copy-done.1, bf16[2048,2816]{1,0:T(8,128)(2,1)S(1)} %bitcast.191), kind=kOutput, calls=%fused_computation.166 | convolution fusion | flops 2952790016 | bytes 15466496 | tf_op jit(solution)/shard_map/dot_general | solution.py:23
  87.0 15.6 %convolution_convert_fusion = bf16[256,2048]{1,0:T(8,128)(2,1)} fusion(bf16[2816,2048]{1,0:T(8,128)(2,1)} %param.22, bf16[256,2048]{1,0:T(8,128)(2,1)S(1)} %copy-done.1, bf16[2048,2816]{1,0:T(8,128)(2,1)} %param.21, f32[256,2816]{1,0:T(8,128)} %fusion.117), kind=kOutput, calls=%fused_computation.84 | convolution fusion | flops 5910429696 | bytes 28049408 | tf_op jit(solution)/shard_map/dot_general | solution.py:26
  102.6 4.8 %fusion.75 = pred[32,256,64]{1,2,0:T(8,128)(4,1)S(1)} fusion(s32[32,256,6]{1,2,0:T(8,128)S(1)} %bitcast.177), kind=kLoop, calls=%fused_computation.70 | loop fusion | flops 5767168 | bytes 720896 | tf_op jit(solution)/shard_map/reduce_or | solution.py:356
  110.6 15.0 %all-gather.2.cloned.1.call-done = bf16[8192,2048]{1,0:T(8,128)(2,1)} async-done(((bf16[256,2048]{1,0:T(8,128)(2,1)}), bf16[8192,2048]{1,0:T(8,128)(2,1)}) %all-gather.2.cloned.1.call-update) | async-done | bytes 33554448 | tf_op jit(solution)/shard_map/all_gather | solution.py:319
  125.5 237.9 %moe_exchange.1 = (f32[256,2048]{1,0:T(8,128)}, bf16[32,96,2048]{2,1,0:T(8,128)(2,1)}, bf16[14,96,2048]{2,1,0:T(8,128)(2,1)}) custom-call(bf16[32,256,2048]{2,1,0:T(8,128)(2,1)} %bitcast.188, bf16[32,128,256]{2,1,0:T(8,128)(2,1)} %fusion.78.pick_ref, bf16[32,96,128]{2,1,0:T(8,128)(2,1)} %fusion.85.pack_ref, bf16[16,768,192]{2,1,0:T(8,128)(2,1)} %pad_maximum_fusion.comb_ref, ...), custom_call_target="tpu_custom_call" | custom-call | flops 70866960384 | bytes 80000000 | tf_op jit(solution)/shard_map/moe_exchange/pallas_call | solution.py:272
  363.4 7.3 %conditional.2 = (f32[256,2048]{1,0:T(8,128)}, f32[256,2048]{1,0:T(8,128)}, f32[256,2048]{1,0:T(8,128)}, bf16[256,2048]{1,0:T(8,128)(2,1)}) conditional(s32[]{:T(128)} %convert_element_type.175, (f32[256,2048]{1,0:T(8,128)}, bf16[256,2048]{1,0:T(8,128)(2,1)}, bf16[256,2048]{1,0:T(8,128)(2,1)}) %tuple.24, (bf16[8192,2048]{1,0:T(8,128)(2,1)}, ...), branch_computations={%region_15.16_spmd, %region_16.26_spmd} | conditional | flops 17810087936 | bytes 309368224
  363.5 2.8 convert_element_type.199
  366.2 3.1 copy.143
  370.7 4.0 %fusion.83 = bf16[256,2048]{1,0:T(8,128)(2,1)} fusion(f32[256,2048]{1,0:T(8,128)} %get-tuple-element.209, f32[256,2048]{1,0:T(8,128)} %get-tuple-element.211, bf16[256,2048]{1,0:T(8,128)(2,1)} %get-tuple-element.212), kind=kLoop, calls=%fused_computation.90 | loop fusion | flops 2097152 | bytes 6291456 | tf_op jit(solution)/shard_map/cond/branch_0_fun/convert_element_type | solution.py:383
  (76 shorter events, 5.1 us)
Async XLA Ops:
  6.5 5.0 %copy-start.10 = (s32[32]{0:T(128)S(1)}, s32[32]{0:T(128)}, u32[]{:S(2)}) copy-start(s32[32]{0:T(128)} %constant.170.clone) | copy-start | bytes 388
  6.5 5.0 %copy-start.11 = (s32[32]{0:T(128)S(1)}, s32[32]{0:T(128)}, u32[]{:S(2)}) copy-start(s32[32]{0:T(128)} %constant.174) | copy-start | bytes 388
  6.6 5.0 %copy-start.12 = (s32[32]{0:T(128)S(1)}, s32[32]{0:T(128)}, u32[]{:S(2)}) copy-start(s32[32]{0:T(128)} %constant.175) | copy-start | bytes 388
  6.6 5.2 %copy-start.6 = (bf16[2048,64]{0,1:T(8,128)(2,1)S(1)}, bf16[2048,64]{0,1:T(8,128)(2,1)}, u32[]{:S(2)}) copy-start(bf16[2048,64]{0,1:T(8,128)(2,1)} %param.19) | copy-start | bytes 786436
  6.6 7.1 %copy-start.7 = (s32[256,6]{0,1:T(8,128)S(1)}, s32[256,6]{0,1:T(8,128)}, u32[]{:S(2)}) copy-start(s32[256,6]{0,1:T(8,128)} %param.26) | copy-start | bytes 18436
  6.6 119.0 %all-gather.2.cloned.1.call-start = ((), (), s32[]{:S(2)}) async-start(), calls=%async_computation.2 | async-start | bytes 34603008 | tf_op jit(solution)/shard_map/all_gather | solution.py:319
  60.0 42.5 %copy-start.4 = (s32[8192,6]{0,1:T(8,128)}, s32[8192,6]{0,1:T(8,128)S(1)}, u32[]{:S(2)}) copy-start(s32[8192,6]{0,1:T(8,128)S(1)} %all_gather.9) | copy-start | bytes 589828
  60.1 4.8 %copy-start.8 = (s32[32]{0:T(128)S(1)}, s32[32]{0:T(128)}, u32[]{:S(2)}) copy-start(s32[32]{0:T(128)} %constant.168.clone) | copy-start | bytes 388
  60.1 4.8 %copy-start.9 = (s32[32]{0:T(128)S(1)}, s32[32]{0:T(128)}, u32[]{:S(2)}) copy-start(s32[32]{0:T(128)} %constant.169.clone) | copy-start | bytes 388
  69.8 12.4 %slice-start = ((s8[11534336]{0:T(1024)(128)(4,1)}), s8[4194304]{0:T(1024)(128)(4,1)S(1)}, s32[]{:S(2)}) async-start(s8[11534336]{0:T(1024)(128)(4,1)} %bitcast.190), calls=%async_computation.3 | async-start | bytes 8388608
  69.8 12.4 %slice-start.1 = ((s8[11534336]{0:T(1024)(128)(4,1)}), s8[4194304]{0:T(1024)(128)(4,1)S(1)}, s32[]{:S(2)}) async-start(s8[11534336]{0:T(1024)(128)(4,1)} %bitcast.190), calls=%async_computation.4 | async-start | bytes 8388608
  75.9 6.3 %copy-start.1 = (bf16[256,2048]{1,0:T(8,128)(2,1)S(1)}, bf16[256,2048]{1,0:T(8,128)(2,1)}, u32[]{:S(2)}) copy-start(bf16[256,2048]{1,0:T(8,128)(2,1)} %fusion.82) | copy-start | bytes 3145732
  75.9 6.3 %slice-start.2 = ((s8[11534336]{0:T(1024)(128)(4,1)}), s8[3145728]{0:T(1024)(128)(4,1)S(1)}, s32[]{:S(2)}) async-start(s8[11534336]{0:T(1024)(128)(4,1)} %bitcast.190), calls=%async_computation.5 | async-start | bytes 6291456
Sparse Core Ops, SparseCore 0:
  11.6 113.8 all-gather.1
where the time goes:
time: 386 us; the launch traced here: 382 us
  Pallas kernels  238 us (62%)
  other arithmetic  37.6 us (10%)
  blocking collectives  34.1 us (9%)
  matrix products  22.8 us (6%)
  local copies, waits for them, and re-layouts  17.5 us (5%)
  between operations  15.4 us (4%)
  waiting for transfers between devices  15 us (4%)
    pallas_call x1, Pallas kernels, expert_exchange(): pl.pallas_call(functools.partial(moe_kernel, n, cap_e, cap), out_shape=(j...  238 us
    all_gather x1, blocking collectives, local_fn(): all_ids = lax.all_gather(topk_ids, 'ep', axis=0, tiled=True)  34.1 us
    dot_general x1, matrix products, swiglu(): jnp.dot(inner_act, w_down, preferred_element_type=jnp.float32)  15.6 us
    all_gather x1, waiting for transfers between devices, local_fn(): all_rows = lax.all_gather(normed, 'ep', axis=0, tiled=True)  15 us
  transfers between devices with their start and end apart: 1, of which 1 were waited for; matrix products, arithmetic and copies ran while one was open for 17% of the time, Pallas kernels for 0%

commit v1 on v0

--- a/solution.py
+++ b/solution.py
@@ -67,7 +67,7 @@
 
 def moe_kernel(n, cap_e, cap, rows_ref, pick_ref, pack_ref, comb_ref, w1_ref, w3_ref, w2_ref,
                sum_ref, recv_ref, relay_ref,
-               w1_v, w3_v, w2_v, row_v, xy_v, h_v, stage_v, w_sem, row_sem, send_sem, recv_sem, relay_sem, pass_sem, got_sem):
+               w1_v, w3_v, wr_v, w2_v, row_v, xy_v, h_v, stage_v, w_sem, row_sem, send_sem, recv_sem, relay_sem, pass_sem, got_sem):
     side, flows, relays = flow_table(n)
     relay_slot = {i: j for j, i in enumerate(relays)}
     tiles = n // QUAD
@@ -75,10 +75,16 @@
     block = rows_ref.shape[1]
     me = lax.axis_index('ep')
 
-    loads = []
-    for e in range(local):
-        for j, (src, dst) in enumerate(((w1_ref, w1_v), (w3_ref, w3_v), (w2_ref, w2_v))):
-            loads.append(pltpu.make_async_copy(src.at[e], dst.at[e], w_sem.at[3 * e + j]))
+    main = w1_v.shape[2]
+    rest = inner - main
+
+    def loads(e):
+        whole, tail = pl.ds(0, main), pl.ds(main, rest)
+        pairs = [(w1_ref.at[e, :, whole], w1_v.at[e]), (w3_ref.at[e, :, whole], w3_v.at[e])]
+        if rest:
+            pairs += [(w1_ref.at[e, :, tail], wr_v.at[e, :, pl.ds(0, rest)]), (w3_ref.at[e, :, tail], wr_v.at[e, :, pl.ds(rest, rest)])]
+        pairs.append((w2_ref.at[e], w2_v.at[e]))
+        return [pltpu.make_async_copy(src, dst, w_sem.at[e, j]) for j, (src, dst) in enumerate(pairs)]
 
     def row_start(t):
         for q in range(QUAD):
@@ -110,16 +116,17 @@
         return pltpu.make_async_copy(staged(t, q), recv_ref.at[t * QUAD + q], recv_sem.at[t * QUAD + q])
 
     row_start(0)
-    for load in loads:
+    for load in loads(0):
         load.start()
+    sum_ref[...] = jnp.zeros_like(sum_ref)
 
     barrier = pltpu.get_barrier_semaphore()
     for off in range(1, n):
         pl.semaphore_signal(barrier, inc=1, device_id={'ep': (me + off) % n}, device_id_type=MESH)
     pl.semaphore_wait(barrier, n - 1)
 
-    def columns(i, width):
-        return pl.ds(pl.multiple_of(i * width, width), width)
+    def pieces(total, width):
+        return [pl.ds(at, min(width, total - at)) for at in range(0, total, width)]
 
     def tile(k, carry):
         slot = k % 2
@@ -130,51 +137,51 @@
 
         for q in range(QUAD):
             pltpu.make_async_copy(rows_ref.at[0], row_v.at[slot, q], row_sem.at[slot, q]).wait()
-            width = min(512, depth)
             pick = pick_ref[k * QUAD + q]
-
-            def gather(i, carry):
-                got = jnp.dot(pick, row_v[slot, q, :, columns(i, width)], preferred_element_type=jnp.float32)
-                got = got.astype(jnp.bfloat16)
+            for at in pieces(depth, 512):
+                got = jnp.dot(pick, row_v[slot, q, :, at], preferred_element_type=jnp.float32).astype(jnp.bfloat16)
                 for e in range(local):
-                    xy_v[e, q * cap_e:(q + 1) * cap_e, columns(i, width)] = got[e * cap_e:(e + 1) * cap_e]
-                return carry
-
-            lax.fori_loop(0, depth // width, gather, 0)
-
-        for e in range(local):
+                    xy_v[e, q * cap_e:(q + 1) * cap_e, at] = got[e * cap_e:(e + 1) * cap_e]
+
+        def expert(e, carry):
             @pl.when(k == 0)
             def _():
-                loads[3 * e].wait()
-                loads[3 * e + 1].wait()
-
-            def up_cols(at):
-                rows_in = xy_v[e]
-                gate_act = jnp.dot(rows_in, w1_v[e, :, at], preferred_element_type=jnp.float32)
-                lin_act = jnp.dot(rows_in, w3_v[e, :, at], preferred_element_type=jnp.float32)
+                for load in loads(e)[:-1]:
+                    load.wait()
+
+                @pl.when(e + 1 < local)
+                def _():
+                    for load in loads(e + 1):
+                        load.start()
+
+            rows_in = xy_v.at[e]
+            for at in pieces(main, 256):
+                gate_act = jnp.dot(rows_in[...], w1_v[e, :, at], preferred_element_type=jnp.float32)
+                lin_act = jnp.dot(rows_in[...], w3_v[e, :, at], preferred_element_type=jnp.float32)
                 h_v[:, at] = (jax.nn.silu(gate_act) * lin_act).astype(jnp.bfloat16)
-
-            def up(i, carry):
-                up_cols(columns(i, 256))
-                return carry
-
-            lax.fori_loop(0, inner // 256, up, 0)
-            if inner % 256:
-                up_cols(pl.ds(inner - inner % 256, inner % 256))
+            if rest:
+                both = jnp.dot(rows_in[...], wr_v[e], preferred_element_type=jnp.float32)
+                h_v[:, main:] = (jax.nn.silu(both[:, :rest]) * both[:, rest:]).astype(jnp.bfloat16)
 
             @pl.when(k == 0)
             def _():
-                loads[3 * e + 2].wait()
+                loads(e)[-1].wait()
+
+            wide = min(1024, depth)
 
             def down(i, carry):
-                at = columns(i, 256)
-                got = jnp.dot(h_v[...], w2_v[e, :, at], preferred_element_type=jnp.float32).astype(jnp.bfloat16)
-                for q in range(QUAD):
-                    row = q * local * cap_e + e * cap_e
-                    xy_v[local + row // (QUAD * cap_e), row % (QUAD * cap_e):row % (QUAD * cap_e) + cap_e, at] = got[q * cap_e:(q + 1) * cap_e]
+                for piece in pieces(wide, 256):
+                    at = pl.ds(pl.multiple_of(i * wide + piece.start, 256), 256)
+                    got = jnp.dot(h_v[...], w2_v[e, :, at], preferred_element_type=jnp.float32).astype(jnp.bfloat16)
+                    for q in range(QUAD):
+                        row = q * local * cap_e
+                        xy_v[local + row // (QUAD * cap_e), pl.ds(pl.multiple_of(row % (QUAD * cap_e) + e * cap_e, cap_e), cap_e), at] = got[q * cap_e:(q + 1) * cap_e]
                 return carry
 
-            lax.fori_loop(0, depth // 256, down, 0)
+            lax.fori_loop(0, depth // wide, down, 0)
+            return carry
+
+        lax.fori_loop(0, local, expert, 0)
 
         for t in range(3, tiles):
             ready = [i for i in relays if i // QUAD == t - 3]
@@ -192,18 +199,11 @@
                 pltpu.make_async_copy(stage_v.at[slot, q], stage_v.at[slot, q], send_sem.at[slot, q]).wait()
 
         for q in range(QUAD):
-            width = min(512, depth)
             pack = pack_ref[k * QUAD + q]
             row = q * local * cap_e
-
-            def compact(i, carry):
-                at = columns(i, width)
+            for at in pieces(depth, 512):
                 y_in = xy_v[local + row // (QUAD * cap_e), row % (QUAD * cap_e):row % (QUAD * cap_e) + local * cap_e, at]
-                got = jnp.dot(pack, y_in, preferred_element_type=jnp.float32)
-                stage_v[slot, q, :, at] = got.astype(jnp.bfloat16)
-                return carry
-
-            lax.fori_loop(0, depth // width, compact, 0)
+                stage_v[slot, q, :, at] = jnp.dot(pack, y_in, preferred_element_type=jnp.float32).astype(jnp.bfloat16)
 
         for t in range(tiles):
             @pl.when(k == t)
@@ -223,35 +223,27 @@
     def got_copy(c, j):
         return pltpu.make_async_copy(recv_ref.at[2 * c + j], xy_v.at[c % slots, pl.ds(j * cap, cap), :], got_sem.at[c % slots, j])
 
-    def add_chunk(c, first):
-        for j in range(2):
-            got_copy(c, j).wait()
-
-        def add(i, carry):
-            at = columns(i, 256)
-            got = jnp.dot(comb_ref[c], xy_v[c % slots, :2 * cap, at], preferred_element_type=jnp.float32)
-            got = got[:block] + (got[block:2 * block] + got[2 * block:])
-            sum_ref[:, at] = got if first else sum_ref[:, at] + got
-            return carry
-
-        lax.fori_loop(0, depth // 256, add, 0)
-
     def fetch(c):
         for j in range(2):
             pltpu.make_async_copy(recv_ref.at[2 * c + j], recv_ref.at[2 * c + j], recv_sem.at[2 * c + j]).wait()
             got_copy(c, j).start()
 
     fetch(0)
-    fetch(1)
-    add_chunk(0, True)
-
-    def step(c, carry):
-        fetch(c + 1)
-        add_chunk(c, False)
+
+    def add_chunk(c, carry):
+        @pl.when(c + 1 < chunks)
+        def _():
+            fetch(c + 1)
+
+        for j in range(2):
+            got_copy(c, j).wait()
+        for at in pieces(depth, 256):
+            got = xy_v[c % slots, :2 * cap, at]
+            parts = [jnp.dot(comb_ref[c, p * block:(p + 1) * block], got, preferred_element_type=jnp.float32) for p in range(3)]
+            sum_ref[:, at] = sum_ref[:, at] + (parts[0] + parts[1] + parts[2])
         return carry
 
-    lax.fori_loop(1, chunks - 1, step, 0)
-    add_chunk(chunks - 1, False)
+    lax.fori_loop(0, chunks, add_chunk, 0)
 
     for i in relays:
         pltpu.make_async_copy(relay_ref.at[relay_slot[i]], relay_ref.at[relay_slot[i]], pass_sem.at[relay_slot[i]]).wait()
@@ -269,6 +261,8 @@
     anyspec = pl.BlockSpec(memory_space=pl.ANY)
     flops = 2 * n * local * cap_e * depth * inner * 3
     passing = len(flow_table(n)[2])
+    main = inner - inner % 256
+    assert inner % 256 in (0, 128)
     return pl.pallas_call(
         functools.partial(moe_kernel, n, cap_e, cap),
         out_shape=(jax.ShapeDtypeStruct((block, depth), jnp.float32),
@@ -277,14 +271,15 @@
         in_specs=[anyspec, vmem, vmem, vmem, anyspec, anyspec, anyspec],
         out_specs=(vmem, anyspec, anyspec),
         scratch_shapes=[
-            pltpu.VMEM(w1.shape, jnp.bfloat16),
-            pltpu.VMEM(w3.shape, jnp.bfloat16),
+            pltpu.VMEM((local, depth, main), jnp.bfloat16),
+            pltpu.VMEM((local, depth, main), jnp.bfloat16),
+            pltpu.VMEM((local, depth, max(256, 2 * (inner - main))), jnp.bfloat16),
             pltpu.VMEM(w2.shape, jnp.bfloat16),
             pltpu.VMEM((2, QUAD, block, depth), jnp.bfloat16),
             pltpu.VMEM((2 * local, QUAD * cap_e, depth), jnp.bfloat16),
             pltpu.VMEM((QUAD * cap_e, inner), jnp.bfloat16),
             pltpu.VMEM((2, QUAD, cap, depth), jnp.bfloat16),
-            pltpu.SemaphoreType.DMA((3 * local,)),
+            pltpu.SemaphoreType.DMA((local, 5)),
             pltpu.SemaphoreType.DMA((2, QUAD)),
             pltpu.SemaphoreType.DMA((2, QUAD)),
             pltpu.SemaphoreType.DMA((n,)),
@@ -359,11 +354,12 @@
         pick, pack, comb3, shared_out = lax.optimization_barrier((pick, pack, comb3, shared_out))
         routed = expert_exchange(n, cap_e, cap, all_rows.reshape(n, block, depth), pick, pack, comb3, w1_experts, w3_experts, w2_experts)
 
-        def correction(rows, row_ids, w1, w3, w2):
+        def correction(carry):
+            total, todo = carry
             probs = jax.nn.softmax(jnp.dot(normed, w_gate, preferred_element_type=jnp.float32), axis=-1)
             wts = lax.all_gather(ROUTE_SCALE * jnp.take_along_axis(probs, topk_ids, axis=1), 'ep', axis=0, tiled=True)
-            row_w = jnp.sum(jnp.where(row_ids[:, :, None] == local_ids, wts[:, :, None], 0.0), axis=1)
-            mask = jnp.any(row_ids[:, :, None] == local_ids, axis=1).astype(jnp.float32).reshape(n, block, 1, local)
+            row_w = jnp.sum(jnp.where(all_ids[:, :, None] == local_ids, wts[:, :, None], 0.0), axis=1)
+            mask = jnp.any(all_ids[:, :, None] == local_ids, axis=1).astype(jnp.float32).reshape(n, block, 1, local)
             rank, _, _, start = assign_slots(mask, cap_e)
             left = (mask > 0) & ~((rank < cap_e) & (rank + start[:, None] < cap))
             row_w = jnp.where(left.reshape(n * block, local), row_w, 0.0)
@@ -373,16 +369,13 @@
                 r, w = chunk
                 acc = jnp.zeros(r.shape, jnp.float32)
                 for e in range(local):
-                    acc = acc + w[:, e:e + 1] * swiglu(r, w1[e], w3[e], w2[e]).astype(jnp.float32)
+                    acc = acc + w[:, e:e + 1] * swiglu(r, w1_experts[e], w3_experts[e], w2_experts[e]).astype(jnp.float32)
                 return acc
 
-            part = lax.map(step, (rows.reshape(chunks, -1, depth), row_w.reshape(chunks, -1, local))).reshape(n * block, depth)
-            return lax.psum_scatter(part, 'ep', scatter_dimension=0, tiled=True)
-
-        def finish(total):
-            return (hidden.astype(jnp.float32) + shared_out.astype(jnp.float32) + total).astype(jnp.bfloat16)
-
-        return lax.cond(over, lambda *args: finish(routed + correction(*args)), lambda *args: finish(routed),
-                        all_rows, all_ids, w1_experts, w3_experts, w2_experts)
+            part = lax.map(step, (all_rows.reshape(chunks, -1, depth), row_w.reshape(chunks, -1, local))).reshape(n * block, depth)
+            return total + lax.psum_scatter(part, 'ep', scatter_dimension=0, tiled=True), jnp.logical_and(todo, False)
+
+        routed = lax.while_loop(lambda carry: carry[1], correction, (routed, over))[0]
+        return (hidden.astype(jnp.float32) + shared_out.astype(jnp.float32) + routed).astype(jnp.bfloat16)
 
     return jax.shard_map(local_fn, mesh=mesh, in_specs=(tok_spec, P(), P(), P(), P(), P(), expert_spec, expert_spec, expert_spec, tok_spec), out_specs=tok_spec, check_vma=False)

time: 386 us -> 333 us (0.86)
  Pallas kernels: 238 us -> 192 us
    pallas_call x1, Pallas kernels: 238 us -> 192 us  [expert_exchange(): pl.pallas_call(functools.partial(moe_kernel, n, cap_e, cap), out_shape=(j...]
  transfers between devices with their start and end apart: 1 -> 1, of which waited for: 1 -> 1; matrix products, arithmetic and copies ran while one was open for 17% -> 19% of each run, Pallas kernels for 0% -> 0%
where the time goes in v1:
time: 333 us; the launch traced here: 329 us
  Pallas kernels  192 us (58%)
  blocking collectives  34.3 us (10%)
  other arithmetic  34 us (10%)
  matrix products  22.8 us (7%)
  between operations  15.3 us (5%)
  local copies, waits for them, and re-layouts  15.2 us (5%)
  waiting for transfers between devices  14.3 us (4%)
    pallas_call x1, Pallas kernels, expert_exchange(): pl.pallas_call(functools.partial(moe_kernel, n, cap_e, cap), out_shape=(j...  192 us
    all_gather x1, blocking collectives, local_fn(): all_ids = lax.all_gather(topk_ids, 'ep', axis=0, tiled=True)  34.3 us
    dot_general x1, matrix products, swiglu(): jnp.dot(inner_act, w_down, preferred_element_type=jnp.float32)  15.6 us
    all_gather x1, waiting for transfers between devices, local_fn(): all_rows = lax.all_gather(normed, 'ep', axis=0, tiled=True)  14.3 us
  transfers between devices with their start and end apart: 1, of which 1 were waited for; matrix products, arithmetic and copies ran while one was open for 19% of the time, Pallas kernels for 0%

profile of v1, /device:TPU:97, one launch (start us, length us, event | category | flops | bytes accessed | tf_op | source)
XLA Modules:
  0.0 329.2 jit_solution(11330517843562177213)
XLA Ops:
  6.6 0.7 convert_element_type.175
  7.4 1.5 fusion.85
  8.9 2.5 fusion.87
  11.8 0.8 copy.97
  12.5 1.8 fusion.122
  15.4 1.0 select_reduce_fusion
  16.4 2.0 bitcast_reduce-precision_fusion
  18.3 5.0 %copy.92 = f32[16,256,192]{2,1,0:T(8,128)} copy(f32[16,256,192]{1,2,0:T(8,128)} %bitcast_reduce-precision_fusion) | data formatting | bytes 6291456 | tf_op jit(solution)/shard_map/reduce_precision | solution.py:297
  23.3 3.4 %copy.93 = f32[16,256,192]{2,1,0:T(8,128)} copy(f32[16,256,192]{1,2,0:T(8,128)S(1)} %bitcast.177) | data formatting | bytes 6291456 | tf_op jit(solution)/shard_map/reshape | solution.py:334
  26.7 34.3 %all_gather.9 = s32[8192,6]{0,1:T(8,128)S(1)} all-gather(s32[256,6]{0,1:T(8,128)S(1)} %copy-done.8), channel_id=1, replica_groups=mesh['dp'=1,'ep'=32] {'ep'}, dimensions={0}, use_global_device_ids=true | all-gather | bytes 202752 | tf_op jit(solution)/shard_map/all_gather | solution.py:315
  61.0 1.1 copy.81
  62.1 3.3 convert_element_type.165
  67.4 2.1 fusion.83.pick_ref
  69.5 1.2 fusion.91.pack_ref
  70.7 6.1 %reduce-precision_convert_fusion = (bf16[16,256,192]{2,1,0:T(8,128)(2,1)S(1)}, bf16[16,256,192]{2,1,0:T(8,128)(2,1)S(1)}, bf16[16,256,192]{2,1,0:T(8,128)(2,1)S(1)}) fusion(f32[16,256,192]{2,1,0:T(8,128)} %copy.93, f32[16,256,192]{2,1,0:T(8,128)} %copy.92), kind=kLoop, calls=%fused_computation.79 | loop fusion | flops 4718592 | bytes 11010048 | tf_op jit(solution)/shard_map/convert_element_type | solution.py:300
  76.8 6.2 %pad_maximum_fusion.comb_ref = bf16[16,768,192]{2,1,0:T(8,128)(2,1)} fusion(bf16[16,256,192]{2,1,0:T(8,128)(2,1)S(1)} %get-tuple-element.251, bf16[16,256,192]{2,1,0:T(8,128)(2,1)S(1)} %get-tuple-element.250, bf16[16,256,192]{2,1,0:T(8,128)(2,1)S(1)} %get-tuple-element.252), kind=kLoop, calls=%fused_computation.75 | loop fusion | flops 14155776 | bytes 9437184 | tf_op jit(solution)/shard_map/concatenate | solution.py:335
  83.0 4.8 %fusion.123 = f32[256,2816]{1,0:T(8,128)} fusion(bf16[256,2048]{1,0:T(8,128)(2,1)S(1)} %copy-done.2, bf16[2048,2816]{1,0:T(8,128)(2,1)S(1)} %bitcast.192), kind=kOutput, calls=%fused_computation.171 | convolution fusion | flops 2952790016 | bytes 15466496 | tf_op jit(solution)/shard_map/dot_general | solution.py:23
  87.8 15.6 %convolution_convert_fusion = bf16[256,2048]{1,0:T(8,128)(2,1)} fusion(bf16[2816,2048]{1,0:T(8,128)(2,1)} %param.22, bf16[256,2048]{1,0:T(8,128)(2,1)S(1)} %copy-done.2, bf16[2048,2816]{1,0:T(8,128)(2,1)} %param.21, f32[256,2816]{1,0:T(8,128)} %fusion.123), kind=kOutput, calls=%fused_computation.89 | convolution fusion | flops 5910429696 | bytes 28049408 | tf_op jit(solution)/shard_map/dot_general | solution.py:26
  103.4 4.8 %fusion.80 = pred[32,256,64]{1,2,0:T(8,128)(4,1)S(1)} fusion(s32[32,256,6]{1,2,0:T(8,128)S(1)} %bitcast.175), kind=kLoop, calls=%fused_computation.74 | loop fusion | flops 5767168 | bytes 720896 | tf_op jit(solution)/shard_map/reduce_or | solution.py:351
  108.8 0.7 compare_reduce_fusion.4
  111.3 14.3 %all-gather.2.cloned.1.call-done = bf16[8192,2048]{1,0:T(8,128)(2,1)} async-done(((bf16[256,2048]{1,0:T(8,128)(2,1)}), bf16[8192,2048]{1,0:T(8,128)(2,1)}) %all-gather.2.cloned.1.call-update) | async-done | bytes 33554448 | tf_op jit(solution)/shard_map/all_gather | solution.py:314
  125.6 191.8 %moe_exchange.1 = (f32[256,2048]{1,0:T(8,128)}, bf16[32,96,2048]{2,1,0:T(8,128)(2,1)}, bf16[14,96,2048]{2,1,0:T(8,128)(2,1)}) custom-call(bf16[32,256,2048]{2,1,0:T(8,128)(2,1)} %bitcast.188, bf16[32,128,256]{2,1,0:T(8,128)(2,1)} %fusion.83.pick_ref, bf16[32,96,128]{2,1,0:T(8,128)(2,1)} %fusion.91.pack_ref, bf16[16,768,192]{2,1,0:T(8,128)(2,1)} %pad_maximum_fusion.comb_ref, ...), custom_call_target="tpu_custom_call" | custom-call | flops 70866960384 | bytes 80000000 | tf_op jit(solution)/shard_map/moe_exchange/pallas_call | solution.py:266
  317.4 1.4 while.20
  318.8 3.3 fusion.89
  (76 shorter events, 4.3 us)
Async XLA Ops:
  6.5 5.0 %copy-start.11 = (s32[32]{0:T(128)S(1)}, s32[32]{0:T(128)}, u32[]{:S(2)}) copy-start(s32[32]{0:T(128)} %constant.170.clone) | copy-start | bytes 388
  6.5 5.0 %copy-start.12 = (s32[32]{0:T(128)S(1)}, s32[32]{0:T(128)}, u32[]{:S(2)}) copy-start(s32[32]{0:T(128)} %constant.174) | copy-start | bytes 388
  6.6 5.0 %copy-start.13 = (s32[32]{0:T(128)S(1)}, s32[32]{0:T(128)}, u32[]{:S(2)}) copy-start(s32[32]{0:T(128)} %constant.175) | copy-start | bytes 388
  6.6 5.2 %copy-start.8 = (s32[256,6]{0,1:T(8,128)S(1)}, s32[256,6]{0,1:T(8,128)}, u32[]{:S(2)}) copy-start(s32[256,6]{0,1:T(8,128)} %param.26) | copy-start | bytes 18436
  6.6 6.0 %copy-start.7 = (bf16[2048,64]{0,1:T(8,128)(2,1)S(1)}, bf16[2048,64]{0,1:T(8,128)(2,1)}, u32[]{:S(2)}) copy-start(bf16[2048,64]{0,1:T(8,128)(2,1)} %param.19) | copy-start | bytes 786436
  6.6 119.0 %all-gather.2.cloned.1.call-start = ((), (), s32[]{:S(2)}) async-start(), calls=%async_computation.1 | async-start | bytes 34603008 | tf_op jit(solution)/shard_map/all_gather | solution.py:314
  26.7 39.1 %copy-start.9 = (s32[32]{0:T(128)S(1)}, s32[32]{0:T(128)}, u32[]{:S(2)}) copy-start(s32[32]{0:T(128)} %constant.168.clone) | copy-start | bytes 388
  26.7 39.1 %copy-start.10 = (s32[32]{0:T(128)S(1)}, s32[32]{0:T(128)}, u32[]{:S(2)}) copy-start(s32[32]{0:T(128)} %constant.169.clone) | copy-start | bytes 388
  61.0 42.5 %copy-start.3 = (s32[8192,6]{0,1:T(8,128)}, s32[8192,6]{0,1:T(8,128)S(1)}, u32[]{:S(2)}) copy-start(s32[8192,6]{0,1:T(8,128)S(1)} %all_gather.9) | copy-start | bytes 589828
  70.7 12.3 %slice-start = ((s8[11534336]{0:T(1024)(128)(4,1)}), s8[4194304]{0:T(1024)(128)(4,1)S(1)}, s32[]{:S(2)}) async-start(s8[11534336]{0:T(1024)(128)(4,1)} %bitcast.191), calls=%async_computation.3 | async-start | bytes 8388608
  70.7 12.3 %slice-start.1 = ((s8[11534336]{0:T(1024)(128)(4,1)}), s8[4194304]{0:T(1024)(128)(4,1)S(1)}, s32[]{:S(2)}) async-start(s8[11534336]{0:T(1024)(128)(4,1)} %bitcast.191), calls=%async_computation.4 | async-start | bytes 8388608
  76.8 6.3 %copy-start.2 = (bf16[256,2048]{1,0:T(8,128)(2,1)S(1)}, bf16[256,2048]{1,0:T(8,128)(2,1)}, u32[]{:S(2)}) copy-start(bf16[256,2048]{1,0:T(8,128)(2,1)} %fusion.87) | copy-start | bytes 3145732
  76.8 6.3 %slice-start.2 = ((s8[11534336]{0:T(1024)(128)(4,1)}), s8[3145728]{0:T(1024)(128)(4,1)S(1)}, s32[]{:S(2)}) async-start(s8[11534336]{0:T(1024)(128)(4,1)} %bitcast.191), calls=%async_computation.5 | async-start | bytes 6291456
  317.4 1.4 copy-start.6
Sparse Core Ops, SparseCore 0:
  11.6 113.9 all-gather.1

commit v2 on v1

--- a/solution.py
+++ b/solution.py
@@ -41,20 +41,15 @@
 def flow_table(n):
     side = next(s for s in range(1, n + 1) if 2 * s * s >= n)
     flows = [(2, 2, 0), (2, 2, 1), (1, 3, 0), (3, 1, 0),
+             (2, 1, 0), (2, 3, 0), (1, 2, 0), (3, 2, 0),
+             (2, 1, 1), (2, 3, 1), (1, 2, 1), (3, 2, 1),
              (2, 0, 0), (2, 0, 1), (0, 2, 0), (0, 2, 1),
-             (2, 1, 0), (2, 1, 1), (1, 2, 0), (1, 2, 1),
-             (2, 3, 0), (2, 3, 1), (3, 2, 0), (3, 2, 1),
-             (1, 0, 0), (3, 0, 0), (0, 1, 0), (0, 3, 0),
-             (1, 0, 1), (3, 0, 1), (0, 1, 1), (0, 3, 1),
              (1, 1, 0), (3, 3, 0), (1, 1, 1), (3, 3, 1),
-             (1, 3, 1), (3, 1, 1), (0, 0, 1), (0, 0, 0)]
+             (1, 3, 1), (3, 1, 1), (0, 1, 0), (0, 3, 0),
+             (1, 0, 0), (3, 0, 0), (0, 1, 1), (0, 3, 1),
+             (1, 0, 1), (3, 0, 1), (0, 0, 1), (0, 0, 0)]
     assert len(set(flows)) == n and side == 4
-    relays = {}
-    for i, (dx, dy, dc) in enumerate(flows):
-        if 2 in (dx, dy):
-            turn = 3 if dc else 1
-            relays[i] = (turn if dx == 2 else 0, turn if dy == 2 else 0)
-    return side, flows, relays
+    return side, flows
 
 
 def device_at(me, side, step, sign=1):
@@ -65,11 +60,10 @@
     return (line * side + col) * 2 + (me + dc) % 2
 
 
-def moe_kernel(n, cap_e, cap, rows_ref, pick_ref, pack_ref, comb_ref, w1_ref, w3_ref, w2_ref,
-               sum_ref, recv_ref, relay_ref,
-               w1_v, w3_v, wr_v, w2_v, row_v, xy_v, h_v, stage_v, w_sem, row_sem, send_sem, recv_sem, relay_sem, pass_sem, got_sem):
-    side, flows, relays = flow_table(n)
-    relay_slot = {i: j for j, i in enumerate(relays)}
+def moe_kernel(n, cap_e, cap, rows_ref, pick_ref, pack_ref, comb_hbm, w1_ref, w3_ref, w2_ref,
+               sum_ref, recv_ref,
+               w1_v, w3_v, wr_v, w2_v, row_v, xy_v, h_v, stage_v, comb_ref, w_sem, row_sem, send_sem, recv_sem, got_sem, comb_sem):
+    side, flows = flow_table(n)
     tiles = n // QUAD
     local, depth, inner = w1_ref.shape
     block = rows_ref.shape[1]
@@ -96,21 +90,9 @@
 
     def send_copy(t, q):
         i = t * QUAD + q
-        if i in relays:
-            ax, ay = relays[i]
-            j = relay_slot[i]
-            dst, sem, to = relay_ref.at[j], relay_sem.at[j], device_at(me, side, (ax, ay, 0))
-        else:
-            dst, sem, to = recv_ref.at[i], recv_sem.at[i], device_at(me, side, flows[i])
         return pltpu.make_async_remote_copy(
-            src_ref=staged(t, q), dst_ref=dst, send_sem=send_sem.at[t % 2, q], recv_sem=sem,
-            device_id={'ep': to}, device_id_type=MESH)
-
-    def pass_copy(i):
-        (ax, ay), (dx, dy, dc), j = relays[i], flows[i], relay_slot[i]
-        return pltpu.make_async_remote_copy(
-            src_ref=relay_ref.at[j], dst_ref=recv_ref.at[i], send_sem=pass_sem.at[j], recv_sem=recv_sem.at[i],
-            device_id={'ep': device_at(me, side, (dx - ax + side, dy - ay + side, dc))}, device_id_type=MESH)
+            src_ref=staged(t, q), dst_ref=recv_ref.at[i], send_sem=send_sem.at[t % 2, q], recv_sem=recv_sem.at[i],
+            device_id={'ep': device_at(me, side, flows[i])}, device_id_type=MESH)
 
     def self_copy(t, q):
         return pltpu.make_async_copy(staged(t, q), recv_ref.at[t * QUAD + q], recv_sem.at[t * QUAD + q])
@@ -142,6 +124,10 @@
                 got = jnp.dot(pick, row_v[slot, q, :, at], preferred_element_type=jnp.float32).astype(jnp.bfloat16)
                 for e in range(local):
                     xy_v[e, q * cap_e:(q + 1) * cap_e, at] = got[e * cap_e:(e + 1) * cap_e]
+
+        @pl.when(k == 2)
+        def _():
+            pltpu.make_async_copy(comb_hbm, comb_ref, comb_sem).start()
 
         def expert(e, carry):
             @pl.when(k == 0)
@@ -182,16 +168,6 @@
             return carry
 
         lax.fori_loop(0, local, expert, 0)
-
-        for t in range(3, tiles):
-            ready = [i for i in relays if i // QUAD == t - 3]
-            if ready:
-                @pl.when(k == t)
-                def _():
-                    for i in ready:
-                        pltpu.make_async_copy(
-                            relay_ref.at[relay_slot[i]], relay_ref.at[relay_slot[i]], relay_sem.at[relay_slot[i]]).wait()
-                        pass_copy(i).start()
 
         @pl.when(k >= 2)
         def _():
@@ -217,6 +193,8 @@
 
     lax.fori_loop(0, tiles, tile, 0)
 
+    pltpu.make_async_copy(comb_hbm, comb_ref, comb_sem).wait()
+
     slots = 2 * local
     chunks = n // 2
 
@@ -245,8 +223,6 @@
 
     lax.fori_loop(0, chunks, add_chunk, 0)
 
-    for i in relays:
-        pltpu.make_async_copy(relay_ref.at[relay_slot[i]], relay_ref.at[relay_slot[i]], pass_sem.at[relay_slot[i]]).wait()
     for t in range(tiles - 2, tiles):
         for q in range(QUAD):
             if flows[t * QUAD + q] != (0, 0, 0):
@@ -260,16 +236,14 @@
     vmem = pl.BlockSpec(memory_space=pltpu.VMEM)
     anyspec = pl.BlockSpec(memory_space=pl.ANY)
     flops = 2 * n * local * cap_e * depth * inner * 3
-    passing = len(flow_table(n)[2])
     main = inner - inner % 256
     assert inner % 256 in (0, 128)
     return pl.pallas_call(
         functools.partial(moe_kernel, n, cap_e, cap),
         out_shape=(jax.ShapeDtypeStruct((block, depth), jnp.float32),
-                   jax.ShapeDtypeStruct((n, cap, depth), jnp.bfloat16),
-                   jax.ShapeDtypeStruct((passing, cap, depth), jnp.bfloat16)),
-        in_specs=[anyspec, vmem, vmem, vmem, anyspec, anyspec, anyspec],
-        out_specs=(vmem, anyspec, anyspec),
+                   jax.ShapeDtypeStruct((n, cap, depth), jnp.bfloat16)),
+        in_specs=[anyspec, vmem, vmem, anyspec, anyspec, anyspec, anyspec],
+        out_specs=(vmem, anyspec),
         scratch_shapes=[
             pltpu.VMEM((local, depth, main), jnp.bfloat16),
             pltpu.VMEM((local, depth, main), jnp.bfloat16),
@@ -279,13 +253,13 @@
             pltpu.VMEM((2 * local, QUAD * cap_e, depth), jnp.bfloat16),
             pltpu.VMEM((QUAD * cap_e, inner), jnp.bfloat16),
             pltpu.VMEM((2, QUAD, cap, depth), jnp.bfloat16),
+            pltpu.VMEM(comb.shape, jnp.bfloat16),
             pltpu.SemaphoreType.DMA((local, 5)),
             pltpu.SemaphoreType.DMA((2, QUAD)),
             pltpu.SemaphoreType.DMA((2, QUAD)),
             pltpu.SemaphoreType.DMA((n,)),
-            pltpu.SemaphoreType.DMA((passing,)),
-            pltpu.SemaphoreType.DMA((passing,)),
             pltpu.SemaphoreType.DMA((2 * local, 2)),
+            pltpu.SemaphoreType.DMA,
         ],
         compiler_params=pltpu.CompilerParams(collective_id=0, has_side_effects=True, vmem_limit_bytes=67_000_000),
         cost_estimate=pl.CostEstimate(flops=flops, bytes_accessed=80_000_000, transcendentals=0),
@@ -315,7 +289,7 @@
         all_ids = lax.all_gather(topk_ids, 'ep', axis=0, tiled=True)
 
         me = lax.axis_index('ep')
-        side, flows, _ = flow_table(n)
+        side, flows = flow_table(n)
         steps = tuple(jnp.array([flow[i] for flow in flows]) for i in range(3))
         dest = device_at(me, side, steps)
         src = device_at(me, side, steps, -1)
@@ -363,17 +337,23 @@
             rank, _, _, start = assign_slots(mask, cap_e)
             left = (mask > 0) & ~((rank < cap_e) & (rank + start[:, None] < cap))
             row_w = jnp.where(left.reshape(n * block, local), row_w, 0.0)
-            chunks = 16
-
-            def step(chunk):
-                r, w = chunk
-                acc = jnp.zeros(r.shape, jnp.float32)
-                for e in range(local):
-                    acc = acc + w[:, e:e + 1] * swiglu(r, w1_experts[e], w3_experts[e], w2_experts[e]).astype(jnp.float32)
-                return acc
-
-            part = lax.map(step, (all_rows.reshape(chunks, -1, depth), row_w.reshape(chunks, -1, local))).reshape(n * block, depth)
-            return total + lax.psum_scatter(part, 'ep', scatter_dimension=0, tiled=True), jnp.logical_and(todo, False)
+            chunks = n * block // 128
+
+            def step(i, part):
+                e, at = i % local, (i // local) * (n * block // chunks)
+                got = swiglu(lax.dynamic_slice_in_dim(all_rows, at, n * block // chunks), w1_experts[e], w3_experts[e], w2_experts[e])
+                wts = jnp.sum(jnp.where(jnp.arange(local) == e, lax.dynamic_slice_in_dim(row_w, at, n * block // chunks), 0.0), axis=1)
+                old = lax.dynamic_slice_in_dim(part, at, n * block // chunks)
+                return lax.dynamic_update_slice_in_dim(part, old + wts[:, None] * got.astype(jnp.float32), at, axis=0)
+
+            part = lax.fori_loop(0, chunks * local, step, jnp.zeros((n * block, depth), jnp.float32))
+            part = part.reshape(n, block, depth)
+            ring = [(i, (i + 1) % n) for i in range(n)]
+
+            def hop(i, acc):
+                return lax.ppermute(acc, 'ep', ring) + part[(me - 2 - i + 2 * n) % n]
+
+            return total + lax.fori_loop(0, n - 1, hop, part[(me - 1 + n) % n]), jnp.logical_and(todo, False)
 
         routed = lax.while_loop(lambda carry: carry[1], correction, (routed, over))[0]
         return (hidden.astype(jnp.float32) + shared_out.astype(jnp.float32) + routed).astype(jnp.bfloat16)

time: 333 us -> 329 us (0.988)
  the two profiles are of different devices: /device:TPU:97 before, /device:TPU:110 now
where the time goes in v2:
time: 329 us; the launch traced here: 324 us
  Pallas kernels  191 us (58%)
  blocking collectives  35.5 us (11%)
  other arithmetic  33.9 us (10%)
  matrix products  22.8 us (7%)
  local copies, waits for them, and re-layouts  16.4 us (5%)
  between operations  15.2 us (5%)
  waiting for transfers between devices  9.14 us (3%)
    pallas_call x1, Pallas kernels, expert_exchange(): pl.pallas_call(functools.partial(moe_kernel, n, cap_e, cap), out_shape=(j...  191 us
    all_gather x1, blocking collectives, local_fn(): all_ids = lax.all_gather(topk_ids, 'ep', axis=0, tiled=True)  35.5 us
    dot_general x1, matrix products, swiglu(): jnp.dot(inner_act, w_down, preferred_element_type=jnp.float32)  15.6 us
    all_gather x1, waiting for transfers between devices, local_fn(): all_rows = lax.all_gather(normed, 'ep', axis=0, tiled=True)  9.09 us
  transfers between devices with their start and end apart: 1, of which 1 were waited for; matrix products, arithmetic and copies ran while one was open for 20% of the time, Pallas kernels for 0%

profile of v2, /device:TPU:110, one launch (start us, length us, event | category | flops | bytes accessed | tf_op | source)
XLA Modules:
  0.0 323.8 jit_solution(404714529827059578)
XLA Ops:
  6.6 0.7 convert_element_type.187
  7.4 1.5 fusion.68
  8.9 2.5 fusion.70
  11.7 0.8 copy.92
  12.6 1.8 fusion.104
  15.4 1.0 select_reduce_fusion
  16.4 2.0 bitcast_reduce-precision_fusion
  18.4 4.9 %copy.87 = f32[16,256,192]{2,1,0:T(8,128)} copy(f32[16,256,192]{1,2,0:T(8,128)} %bitcast_reduce-precision_fusion) | data formatting | bytes 6291456 | tf_op jit(solution)/shard_map/reduce_precision | solution.py:271
  23.3 3.4 %copy.88 = f32[16,256,192]{2,1,0:T(8,128)} copy(f32[16,256,192]{1,2,0:T(8,128)S(1)} %bitcast.134) | data formatting | bytes 6291456 | tf_op jit(solution)/shard_map/reshape | solution.py:308
  26.8 35.5 %all_gather.9 = s32[8192,6]{0,1:T(8,128)S(1)} all-gather(s32[256,6]{0,1:T(8,128)S(1)} %copy-done.6), channel_id=1, replica_groups=mesh['dp'=1,'ep'=32] {'ep'}, dimensions={0}, use_global_device_ids=true | all-gather | bytes 202752 | tf_op jit(solution)/shard_map/all_gather | solution.py:289
  62.3 1.1 copy.76
  63.4 3.3 %convert_element_type.177 = bf16[32,1536]{1,0:T(8,128)(2,1)S(1)} reshape(bf16[8192,6]{1,0:T(8,128)(2,1)S(1)} %copy.76) | data formatting | bytes 196608 | tf_op jit(solution)/shard_map/convert_element_type | solution.py:313
  68.7 2.1 fusion.66.pick_ref
  70.8 1.2 fusion.74.pack_ref
  72.0 6.1 %reduce-precision_convert_fusion = (bf16[16,256,192]{2,1,0:T(8,128)(2,1)S(1)}, bf16[16,256,192]{2,1,0:T(8,128)(2,1)S(1)}, bf16[16,256,192]{2,1,0:T(8,128)(2,1)S(1)}) fusion(f32[16,256,192]{2,1,0:T(8,128)} %copy.88, f32[16,256,192]{2,1,0:T(8,128)} %copy.87), kind=kLoop, calls=%fused_computation.67 | loop fusion | flops 4718592 | bytes 11010048 | tf_op jit(solution)/shard_map/convert_element_type | solution.py:274
  78.1 6.2 %pad_maximum_fusion.comb_hbm = bf16[16,768,192]{2,1,0:T(8,128)(2,1)} fusion(bf16[16,256,192]{2,1,0:T(8,128)(2,1)S(1)} %get-tuple-element.499, bf16[16,256,192]{2,1,0:T(8,128)(2,1)S(1)} %get-tuple-element.498, bf16[16,256,192]{2,1,0:T(8,128)(2,1)S(1)} %get-tuple-element.500), kind=kLoop, calls=%fused_computation.63 | loop fusion | flops 14155776 | bytes 9437184 | tf_op jit(solution)/shard_map/concatenate | solution.py:309
  84.4 4.8 %fusion.105 = f32[256,2816]{1,0:T(8,128)} fusion(bf16[256,2048]{1,0:T(8,128)(2,1)S(1)} %copy-done, bf16[2048,2816]{1,0:T(8,128)(2,1)S(1)} %bitcast.144), kind=kOutput, calls=%fused_computation.158 | convolution fusion | flops 2952790016 | bytes 15466496 | tf_op jit(solution)/shard_map/dot_general | solution.py:23
  89.2 15.6 %convolution_convert_fusion = bf16[256,2048]{1,0:T(8,128)(2,1)} fusion(bf16[2816,2048]{1,0:T(8,128)(2,1)} %param.24, bf16[256,2048]{1,0:T(8,128)(2,1)S(1)} %copy-done, bf16[2048,2816]{1,0:T(8,128)(2,1)} %param.23, f32[256,2816]{1,0:T(8,128)} %fusion.105), kind=kOutput, calls=%fused_computation.77 | convolution fusion | flops 5910429696 | bytes 28049408 | tf_op jit(solution)/shard_map/dot_general | solution.py:26
  104.8 4.7 %fusion.63 = pred[32,256,64]{1,2,0:T(8,128)(4,1)S(1)} fusion(s32[32,256,6]{1,2,0:T(8,128)S(1)} %bitcast.132), kind=kLoop, calls=%fused_computation.62 | loop fusion | flops 5767168 | bytes 720896 | tf_op jit(solution)/shard_map/reduce_or | solution.py:325
  109.9 0.7 compare_reduce_fusion.4
  112.4 9.1 %all-gather.2.cloned.1.call-done = bf16[8192,2048]{1,0:T(8,128)(2,1)} async-done(((bf16[256,2048]{1,0:T(8,128)(2,1)}), bf16[8192,2048]{1,0:T(8,128)(2,1)}) %all-gather.2.cloned.1.call-update) | async-done | bytes 33554448 | tf_op jit(solution)/shard_map/all_gather | solution.py:288
  121.5 190.8 %moe_exchange.1 = (f32[256,2048]{1,0:T(8,128)}, bf16[32,96,2048]{2,1,0:T(8,128)(2,1)}) custom-call(bf16[32,256,2048]{2,1,0:T(8,128)(2,1)} %bitcast.137, bf16[32,128,256]{2,1,0:T(8,128)(2,1)} %fusion.66.pick_ref, bf16[32,96,128]{2,1,0:T(8,128)(2,1)} %fusion.74.pack_ref, bf16[16,768,192]{2,1,0:T(8,128)(2,1)} %pad_maximum_fusion.comb_hbm, ...), custom_call_target="tpu_custom_call" | custom-call | flops 70866960384 | bytes 80000000 | tf_op jit(solution)/shard_map/moe_exchange/pallas_call | solution.py:241
  312.3 1.2 copy-done.4
  313.5 3.3 %fusion.72 = bf16[256,2048]{1,0:T(8,128)(2,1)} fusion(f32[256,2048]{1,0:T(8,128)} %get-tuple-element.369, bf16[256,2048]{1,0:T(8,128)(2,1)S(1)} %copy-done.4, bf16[256,2048]{1,0:T(8,128)(2,1)} %convolution_convert_fusion), kind=kLoop, calls=%fused_computation.83 | loop fusion | flops 2621440 | bytes 5242880 | tf_op jit(solution)/shard_map/convert_element_type | solution.py:359
  (76 shorter events, 4.3 us)
Async XLA Ops:
  6.5 5.0 %copy-start.9 = (s32[32]{0:T(128)S(1)}, s32[32]{0:T(128)}, u32[]{:S(2)}) copy-start(s32[32]{0:T(128)} %constant.337.clone) | copy-start | bytes 388
  6.5 5.0 %copy-start.10 = (s32[32]{0:T(128)S(1)}, s32[32]{0:T(128)}, u32[]{:S(2)}) copy-start(s32[32]{0:T(128)} %constant.341) | copy-start | bytes 388
  6.6 5.0 %copy-start.11 = (s32[32]{0:T(128)S(1)}, s32[32]{0:T(128)}, u32[]{:S(2)}) copy-start(s32[32]{0:T(128)} %constant.342) | copy-start | bytes 388
  6.6 5.2 %copy-start.6 = (s32[256,6]{0,1:T(8,128)S(1)}, s32[256,6]{0,1:T(8,128)}, u32[]{:S(2)}) copy-start(s32[256,6]{0,1:T(8,128)} %param.28) | copy-start | bytes 18436
  6.6 6.0 %copy-start.5 = (bf16[2048,64]{0,1:T(8,128)(2,1)S(1)}, bf16[2048,64]{0,1:T(8,128)(2,1)}, u32[]{:S(2)}) copy-start(bf16[2048,64]{0,1:T(8,128)(2,1)} %param.21) | copy-start | bytes 786436
  6.6 114.9 %all-gather.2.cloned.1.call-start = ((), (), s32[]{:S(2)}) async-start(), calls=%async_computation | async-start | bytes 34603008 | tf_op jit(solution)/shard_map/all_gather | solution.py:288
  26.8 40.3 %copy-start.7 = (s32[32]{0:T(128)S(1)}, s32[32]{0:T(128)}, u32[]{:S(2)}) copy-start(s32[32]{0:T(128)} %constant.335.clone) | copy-start | bytes 388
  26.8 40.3 %copy-start.8 = (s32[32]{0:T(128)S(1)}, s32[32]{0:T(128)}, u32[]{:S(2)}) copy-start(s32[32]{0:T(128)} %constant.336.clone) | copy-start | bytes 388
  62.3 42.5 %copy-start.1 = (s32[8192,6]{0,1:T(8,128)}, s32[8192,6]{0,1:T(8,128)S(1)}, u32[]{:S(2)}) copy-start(s32[8192,6]{0,1:T(8,128)S(1)} %all_gather.9) | copy-start | bytes 589828
  72.0 12.4 %slice-start = ((s8[11534336]{0:T(1024)(128)(4,1)}), s8[4194304]{0:T(1024)(128)(4,1)S(1)}, s32[]{:S(2)}) async-start(s8[11534336]{0:T(1024)(128)(4,1)} %bitcast.143), calls=%async_computation.1 | async-start | bytes 8388608
  72.0 12.4 %slice-start.1 = ((s8[11534336]{0:T(1024)(128)(4,1)}), s8[4194304]{0:T(1024)(128)(4,1)S(1)}, s32[]{:S(2)}) async-start(s8[11534336]{0:T(1024)(128)(4,1)} %bitcast.143), calls=%async_computation.2 | async-start | bytes 8388608
  78.1 6.3 %copy-start = (bf16[256,2048]{1,0:T(8,128)(2,1)S(1)}, bf16[256,2048]{1,0:T(8,128)(2,1)}, u32[]{:S(2)}) copy-start(bf16[256,2048]{1,0:T(8,128)(2,1)} %fusion.70) | copy-start | bytes 3145732
  78.1 6.3 %slice-start.2 = ((s8[11534336]{0:T(1024)(128)(4,1)}), s8[3145728]{0:T(1024)(128)(4,1)S(1)}, s32[]{:S(2)}) async-start(s8[11534336]{0:T(1024)(128)(4,1)} %bitcast.143), calls=%async_computation.3 | async-start | bytes 6291456
  312.2 1.2 copy-start.4
Sparse Core Ops, SparseCore 0:
  11.6 109.8 all-gather.1
